TPU v7x, 32 devices: a whole 2x2x4 slice. The times are simulated.
32 devices in a mesh: seq: 8 (over z, x), head: 4 (over y, core).
Axes of the slice: x: 2, y: 2, z: 4, core: 2. Of those that a mesh axis runs over, the one named last changes fastest.
Arguments:
- queries: bfloat16 [6144, 8192], P('seq', 'head'), may hold values from -6 to 6
- key_rows: bfloat16 [6144, 8192], P('seq', 'head'), may hold values from -0.5 to 0.5
- value_rows: bfloat16 [6144, 8192], P('seq', 'head'), may hold values from -130 to 130
- log_decay: float32 [64, 6144], P('head', 'seq'), may hold values from -1 to 0
- norm_gain: float32 [8192], P('head'), may hold values from 0.1 to 1.9
- grad_out: bfloat16 [6144, 8192], P('seq', 'head'), may hold values from -13 to 13
Outputs:
- output: bfloat16 [6144, 8192], P('seq', 'head')
- grad_queries: bfloat16 [6144, 8192], P('seq', 'head')
- grad_keys: bfloat16 [6144, 8192], P('seq', 'head')
- grad_values: bfloat16 [6144, 8192], P('seq', 'head')
- grad_gain: float32 [8192], P('head')
All inputs are finite; a program needn't handle non-finite values.
Results may differ from a plain program's by a relative error of at most 0.01.
Values sent between devices are 32-bit elements; how exact they have to be, the bound alone decides.
A program may use at most 192 MiB of HBM per device.

v0:
```python
import functools

import jax
import jax.numpy as jnp
from jax import lax
from jax.experimental import pallas as pl
from jax.experimental.pallas import tpu as pltpu
from jax.sharding import PartitionSpec as P

DH = 128
EPSILON = 1e-06
CHUNK = 256
F32 = jnp.float32
BF16 = jnp.bfloat16
MESH = pl.DeviceIdType.MESH
HIGHEST = lax.Precision.HIGHEST


def mm(left, right, dims):
    return lax.dot_general(left, right, (dims, ((), ())), preferred_element_type=F32)


AB = ((1,), (0,))
ABT = ((1,), (1,))
ATB = ((0,), (0,))


def chunk_cumsum(ld_ref, cum_ref, chunk):
    below = lax.broadcasted_iota(jnp.int32, (chunk, chunk), 0)
    right = lax.broadcasted_iota(jnp.int32, (chunk, chunk), 1)
    tri = (below <= right).astype(F32)
    for j in range(ld_ref.shape[1] // chunk):
        span = slice(j * chunk, (j + 1) * chunk)
        cum_ref[:, span] = lax.dot_general(
            ld_ref[:, span], tri, (AB, ((), ())), precision=HIGHEST, preferred_element_type=F32
        )


def cum_forms(cum_ref, h, j, chunk):
    row = cum_ref[pl.ds(h, 1), j * chunk : (j + 1) * chunk]
    column = jnp.broadcast_to(row, (DH, chunk)).T
    return row, column


def decay_of(row, column):
    chunk = row.shape[1]
    wide = jnp.concatenate([column] * (chunk // DH), axis=1)
    t = lax.broadcasted_iota(jnp.int32, (chunk, chunk), 0)
    s = lax.broadcasted_iota(jnp.int32, (chunk, chunk), 1)
    return jnp.where(t >= s, jnp.exp(wide - row), 0.0)


def remote(src, dst, send, recv, axis, target):
    return pltpu.make_async_remote_copy(
        src_ref=src, dst_ref=dst, send_sem=send, recv_sem=recv,
        device_id={axis: target}, device_id_type=MESH,
    )


def loop(count, body):
    lax.fori_loop(0, count, lambda i, c: (body(i), c)[1], 0)


class Chain:
    def __init__(self, n, reverse, bufs):
        (self.lsend, self.lrecv, self.zsend, self.zrecv, self.xsend, self.xrecv, self.sems) = bufs
        me = lax.axis_index("seq")
        self.partner = me + 1 - 2 * lax.rem(me, 2)
        place = n - 1 - me if reverse else me
        self.later = lax.rem(place, 2)
        self.row = place // 2
        self.first = self.row == 0
        self.last = self.row == n // 2 - 1
        step = -2 if reverse else 2
        self.next = lax.rem(me + step + n, n)

    def leads(self, h):
        return lax.rem(h, 2) != self.later

    def copy_l(self, h):
        return remote(self.lsend.at[h], self.lrecv.at[h], self.sems.at[0, h], self.sems.at[1, h], "seq", self.partner)

    def copy_x(self, h):
        return remote(self.xsend.at[h], self.xrecv.at[h], self.sems.at[2, h], self.sems.at[3, h], "seq", self.partner)

    def copy_z(self, h):
        return remote(self.zsend.at[h], self.zrecv.at[h], self.sems.at[4, h], self.sems.at[5, h], "seq", self.next)

    def start(self):
        @pl.when(self.first)
        def _():
            self.zrecv[...] = jnp.zeros_like(self.zrecv)

    def give(self, h, state, decay):
        self.lsend[h, 0:DH] = state
        self.lsend[h, DH : DH + 8] = jnp.broadcast_to(decay, (8, DH))

        @pl.when(jnp.logical_not(self.leads(h)))
        def _():
            self.copy_l(h).start()

    def step(self, h, state_in):
        @pl.when(self.leads(h))
        def _():
            self.copy_l(h).wait_recv()

            @pl.when(jnp.logical_not(self.first))
            def _():
                self.copy_z(h).wait_recv()

            state = self.zrecv[h]

            @pl.when(self.later == 1)
            def _():
                mid = self.lrecv[h, DH : DH + 1] * state + self.lrecv[h, 0:DH]
                self.xsend[h] = state
                self.copy_x(h).start()
                self.zsend[h] = self.lsend[h, DH : DH + 1] * mid + self.lsend[h, 0:DH]
                state_in[h] = mid

            @pl.when(self.later == 0)
            def _():
                mid = self.lsend[h, DH : DH + 1] * state + self.lsend[h, 0:DH]
                self.xsend[h] = mid
                self.copy_x(h).start()
                self.zsend[h] = self.lrecv[h, DH : DH + 1] * mid + self.lrecv[h, 0:DH]
                state_in[h] = state

            @pl.when(jnp.logical_not(self.last))
            def _():
                self.copy_z(h).start()

    def take(self, h, state_in):
        @pl.when(jnp.logical_not(self.leads(h)))
        def _():
            self.copy_x(h).wait_recv()
            state_in[h] = self.xrecv[h]

    def finish(self, h):
        @pl.when(self.leads(h))
        def _():
            self.copy_x(h).wait_send()

            @pl.when(jnp.logical_not(self.last))
            def _():
                self.copy_z(h).wait_send()

        @pl.when(jnp.logical_not(self.leads(h)))
        def _():
            self.copy_l(h).wait_send()


def main_kernel(
    n, peers, chunk,
    q_hbm, k_hbm, v_hbm, g_hbm, ld_ref, gain_ref,
    q, k, v, g, att, obuf, r_out, cum_ref, gg_out,
    s_out, lc, state_in, sq_acc, in_acc,
    stat_send, stat_recv, gain_send, gain_recv, inv_b, cen_b,
    lsend1, lrecv1, zsend1, zrecv1, xsend1, xrecv1,
    lsend2, lrecv2, zsend2, zrecv2, xsend2, xrecv2,
    load_sem, chain1_sem, chain2_sem, stat_sem, gain_sem,
):
    heads, tokens, _ = q.shape
    chunks = tokens // chunk
    me = lax.axis_index("seq")
    my_head = lax.axis_index("head")
    columns = heads * DH * peers

    def load(i, hbm, vmem, h):
        where = pl.ds(pl.multiple_of(h * DH, DH), DH)
        return pltpu.make_async_copy(hbm.at[:, where], vmem.at[h], load_sem.at[i, h])

    def load_kv(h):
        load(0, k_hbm, k, h).start()
        load(1, v_hbm, v, h).start()

    def load_q(h):
        load(2, q_hbm, q, h).start()

    def load_g(h):
        load(3, g_hbm, g, h).start()

    loop(heads, load_kv)
    loop(heads, load_q)
    loop(heads, load_g)

    barrier = pltpu.get_barrier_semaphore()
    for off in range(1, n):
        pl.semaphore_signal(barrier, inc=1, device_id={"seq": lax.rem(me + off, n)}, device_id_type=MESH)
    for off in range(1, peers):
        pl.semaphore_signal(barrier, inc=1, device_id={"head": lax.rem(my_head + off, peers)}, device_id_type=MESH)
    chunk_cumsum(ld_ref, cum_ref, chunk)
    forward = Chain(n, False, (lsend1, lrecv1, zsend1, zrecv1, xsend1, xrecv1, chain1_sem))
    backward = Chain(n, True, (lsend2, lrecv2, zsend2, zrecv2, xsend2, xrecv2, chain2_sem))
    forward.start()
    backward.start()
    pl.semaphore_wait(barrier, n - 1 + peers - 1)

    def local_state(h):
        load(0, k_hbm, k, h).wait()
        load(1, v_hbm, v, h).wait()
        state = None
        for j in range(chunks):
            span = slice(j * chunk, (j + 1) * chunk)
            _, column = cum_forms(cum_ref, h, j, chunk)
            total = column[chunk - 1 : chunk, :]
            tail = jnp.exp(total - column)
            part = mm((k[h, span].astype(F32) * tail).astype(BF16), v[h, span], ATB)
            lc[h, j] = part
            state = part if j == 0 else jnp.exp(total) * state + part
            decay = total if j == 0 else decay + total
        forward.give(h, state, jnp.exp(decay))

    loop(heads, local_state)

    def intra(h):
        load(2, q_hbm, q, h).wait()
        for j in range(chunks):
            span = slice(j * chunk, (j + 1) * chunk)
            row, column = cum_forms(cum_ref, h, j, chunk)
            scores = mm(q[h, span], k[h, span], ABT)
            weights = (scores * decay_of(row, column)).astype(BF16)
            att[h, span] = mm(weights, v[h, span], AB)

    lag = forward.row * 2 + 1

    def overlap(i):
        @pl.when(i < heads)
        def _():
            intra(i)

        at = i - lag

        @pl.when(jnp.logical_and(at >= 0, at < heads))
        def _():
            forward.step(at, state_in)

    loop(heads + n, overlap)

    sq_acc[...] = jnp.zeros_like(sq_acc)
    in_acc[...] = jnp.zeros_like(in_acc)

    def inter(h):
        load(3, g_hbm, g, h).wait()
        forward.take(h, state_in)
        state = state_in[h]
        gain = gain_ref[pl.ds(h, 1), :]
        for j in range(chunks):
            span = slice(j * chunk, (j + 1) * chunk)
            _, column = cum_forms(cum_ref, h, j, chunk)
            rounded = state.astype(BF16)
            s_out[h, j] = rounded
            whole = att[h, span] + jnp.exp(column) * mm(q[h, span], rounded, AB)
            att[h, span] = whole
            sq_acc[span] += whole * whole
            in_acc[span] += g[h, span].astype(F32) * gain * whole
            if j < chunks - 1:
                state = jnp.exp(column[chunk - 1 : chunk, :]) * state + lc[h, j]

    loop(heads, inter)

    ones = jnp.ones((8, DH), F32)

    def row_sums(acc):
        return lax.dot_general(ones, acc, (ABT, ((), ())), precision=HIGHEST, preferred_element_type=F32)

    upper = lax.broadcasted_iota(jnp.int32, (8, tokens), 0) < 4
    stat_send[...] = jnp.where(upper, row_sums(sq_acc[...]), row_sums(in_acc[...]))

    def stat_copy(off, slot):
        return remote(stat_send, stat_recv.at[slot], stat_sem.at[0, off], stat_sem.at[1, off], "head", lax.rem(my_head + off, peers))

    for off in range(1, peers):
        stat_copy(off, my_head).start()
    stat_recv[my_head] = stat_send[...]
    for off in range(1, peers):
        stat_copy(off, lax.rem(my_head + peers - off, peers)).wait_recv()
    stats = stat_recv[0]
    for i in range(1, peers):
        stats = stats + stat_recv[i]
    inverse = lax.rsqrt(stats[0:1] / columns + EPSILON)
    center = stats[4:5] * inverse / columns
    inv_b[...] = jnp.broadcast_to(inverse, (DH, tokens)).T
    cen_b[...] = jnp.broadcast_to(center, (DH, tokens)).T

    def normalize(h):
        gain = gain_ref[pl.ds(h, 1), :]
        gain_part = jnp.zeros((1, DH), F32)
        state = None
        for j in reversed(range(chunks)):
            span = slice(j * chunk, (j + 1) * chunk)
            _, column = cum_forms(cum_ref, h, j, chunk)
            normed = att[h, span] * inv_b[span]
            obuf[h, span] = (normed * gain).astype(BF16)
            cotangent = g[h, span].astype(F32)
            gain_part = gain_part + jnp.sum(cotangent * normed, axis=0, keepdims=True)
            grad = (inv_b[span] * (cotangent * gain - normed * cen_b[span])).astype(BF16)
            g[h, span] = grad
            part = mm((q[h, span].astype(F32) * jnp.exp(column)).astype(BF16), grad, ATB)
            lc[h, j] = part
            total = column[chunk - 1 : chunk, :]
            state = part if state is None else jnp.exp(total) * state + part
            decay = total if j == chunks - 1 else decay + total
        backward.give(h, state, jnp.exp(decay))
        gain_send[pl.ds(h, 1), :] = gain_part

    loop(heads, normalize)

    def gain_copy(off, slot):
        return remote(gain_send, gain_recv.at[slot], gain_sem.at[0, off], gain_sem.at[1, off], "seq", lax.rem(me + off, n))

    for off in range(1, n):
        gain_copy(off, me).start()
    gain_recv[me] = gain_send[...]

    def gradients(h):
        for j in range(chunks):
            span = slice(j * chunk, (j + 1) * chunk)
            row, column = cum_forms(cum_ref, h, j, chunk)
            decay = decay_of(row, column)
            queries, keys, values, grad = q[h, span], k[h, span], v[h, span], g[h, span]
            weights = (mm(queries, keys, ABT) * decay).astype(BF16)
            grad_weights = (mm(grad, values, ABT) * decay).astype(BF16)
            q[h, span] = (
                mm(grad_weights, keys, AB) + jnp.exp(column) * mm(grad, s_out[h, j], ABT)
            ).astype(BF16)
            att[h, span] = mm(grad_weights, queries, ATB)
            g[h, span] = mm(weights, grad, ATB).astype(BF16)

    back_lag = backward.row * 2 + 1

    def overlap_back(i):
        at = i - back_lag

        @pl.when(jnp.logical_and(at >= 0, at < heads))
        def _():
            backward.step(at, state_in)

        @pl.when(i < heads)
        def _():
            gradients(i)

    loop(heads + n, overlap_back)

    def after(h):
        backward.take(h, state_in)
        state = state_in[h]
        for j in reversed(range(chunks)):
            r_out[h, j] = state.astype(BF16)
            if j > 0:
                _, column = cum_forms(cum_ref, h, j, chunk)
                state = jnp.exp(column[chunk - 1 : chunk, :]) * state + lc[h, j]

    loop(heads, after)

    for off in range(1, n):
        gain_copy(off, lax.rem(me + n - off, n)).wait_recv()
    gain_total = gain_recv[0]
    for i in range(1, n):
        gain_total = gain_total + gain_recv[i]
    gg_out[...] = gain_total

    def finish(h):
        forward.finish(h)
        backward.finish(h)

    loop(heads, finish)
    for off in range(1, peers):
        stat_copy(off, my_head).wait_send()
    for off in range(1, n):
        gain_copy(off, me).wait_send()


def last_kernel(
    chunk, k, v, gq, gk, gv, out, after, cum_ref,
    out_hbm, gq_hbm, gk_hbm, gv_hbm, k_stage, v_stage, store_sem,
):
    heads, tokens, _ = k.shape

    def store(i, vmem, hbm, h):
        where = pl.ds(pl.multiple_of(h * DH, DH), DH)
        return pltpu.make_async_copy(vmem.at[h], hbm.at[:, where], store_sem.at[i, h])

    def copies(h):
        return (
            store(0, out, out_hbm, h), store(1, gq, gq_hbm, h),
            store(2, k_stage, gk_hbm, h), store(3, v_stage, gv_hbm, h),
        )

    def one(h):
        ready = copies(h)
        ready[0].start()
        ready[1].start()
        for j in range(tokens // chunk):
            span = slice(j * chunk, (j + 1) * chunk)
            _, column = cum_forms(cum_ref, h, j, chunk)
            tail = jnp.exp(column[chunk - 1 : chunk, :] - column)
            k_stage[h, span] = (gk[h, span] + tail * mm(v[h, span], after[h, j], ABT)).astype(BF16)
            v_stage[h, span] = (
                gv[h, span].astype(F32) + tail * mm(k[h, span], after[h, j], AB)
            ).astype(BF16)
        ready[2].start()
        ready[3].start()

    def wait(h):
        for copy in copies(h):
            copy.wait()

    loop(heads, one)
    loop(heads, wait)


def on_device(n, peers, queries, key_rows, value_rows, log_decay, norm_gain, grad_out):
    tokens, width = queries.shape
    heads = width // DH
    chunk = CHUNK if tokens % CHUNK == 0 else tokens
    chunks = tokens // chunk
    gain = norm_gain.reshape(heads, DH)
    anywhere = pl.BlockSpec(memory_space=pl.ANY)
    vmem = pl.BlockSpec(memory_space=pltpu.VMEM)
    rows = jax.ShapeDtypeStruct((tokens, width), BF16)
    states = jax.ShapeDtypeStruct((heads, chunks, DH, DH), BF16)
    per_head = lambda *shape, dtype=F32: pltpu.VMEM((heads, *shape), dtype)
    chain = [
        per_head(DH + 8, DH), per_head(DH + 8, DH), per_head(DH, DH),
        per_head(DH, DH), per_head(DH, DH), per_head(DH, DH),
    ]
    dma = pltpu.SemaphoreType.DMA
    by_head = lambda dtype: pltpu.VMEM((heads, tokens, DH), dtype)
    *held, grad_gain = pl.pallas_call(
        functools.partial(main_kernel, n, peers, chunk),
        out_shape=(
            by_head(BF16), by_head(BF16), by_head(BF16), by_head(BF16), by_head(F32), by_head(BF16),
            pltpu.VMEM((heads, chunks, DH, DH), BF16), pltpu.VMEM((heads, tokens), F32),
            jax.ShapeDtypeStruct((heads, DH), F32),
        ),
        in_specs=[anywhere] * 4 + [vmem] * 2,
        out_specs=(vmem,) * 9,
        scratch_shapes=[
            per_head(chunks, DH, DH, dtype=BF16), per_head(chunks, DH, DH), per_head(DH, DH),
            pltpu.VMEM((tokens, DH), F32), pltpu.VMEM((tokens, DH), F32),
            pltpu.VMEM((8, tokens), F32), pltpu.VMEM((peers, 8, tokens), F32),
            pltpu.VMEM((heads, DH), F32), pltpu.VMEM((n, heads, DH), F32),
            pltpu.VMEM((tokens, DH), F32), pltpu.VMEM((tokens, DH), F32),
            *chain, *chain,
            dma((4, heads)), dma((6, heads)), dma((6, heads)),
            dma((2, peers)), dma((2, n)),
        ],
        compiler_params=pltpu.CompilerParams(
            collective_id=0, has_side_effects=True, vmem_limit_bytes=32 * 1024 * 1024
        ),
        name="forward_chain",
    )(queries, key_rows, value_rows, grad_out, log_decay, gain)
    grad_q, key_held, value_held, grad_v, grad_k, out, after, cumulative = held
    out, grad_q, grad_k, grad_v = pl.pallas_call(
        functools.partial(last_kernel, chunk),
        out_shape=(rows,) * 4,
        in_specs=[vmem] * 8,
        out_specs=(anywhere,) * 4,
        scratch_shapes=[
            per_head(tokens, DH, dtype=BF16), per_head(tokens, DH, dtype=BF16), dma((4, heads)),
        ],
        compiler_params=pltpu.CompilerParams(vmem_limit_bytes=16 * 1024 * 1024),
        name="last_terms",
    )(key_held, value_held, grad_q, grad_k, grad_v, out, after, cumulative)
    return out, grad_q, grad_k, grad_v, grad_gain.reshape(width)


def solution(mesh):
    in_specs = (
        P("seq", "head"),
        P("seq", "head"),
        P("seq", "head"),
        P("head", "seq"),
        P("head"),
        P("seq", "head"),
    )
    out_specs = (P("seq", "head"), P("seq", "head"), P("seq", "head"), P("seq", "head"), P("head"))
    return jax.shard_map(
        functools.partial(on_device, mesh.shape["seq"], mesh.shape["head"]),
        mesh=mesh, in_specs=in_specs, out_specs=out_specs, check_vma=False,
    )
```

profile of v0, /device:TPU:0, one launch (start us, length us, event | category | flops | bytes accessed | tf_op | source)
XLA Modules:
  0.0 92.9 jit_solution(2203372175538669324)
XLA Ops:
  0.6 86.2 %forward_chain.1 = (bf16[16,768,128]{2,1,0:T(8,128)(2,1)S(1)}, bf16[16,768,128]{2,1,0:T(8,128)(2,1)S(1)}, bf16[16,768,128]{2,1,0:T(8,128)(2,1)S(1)}, bf16[16,768...) custom-call(bf16[768,2048]{1,0:T(8,128)(2,1)} %q_hbm.1, ...), custom_call_target="tpu_custom_call" | custom-call | tf_op jit(solution)/shard_map/forward_chain/pallas_call | solution.py:430
  86.8 0.0 copy-start
  86.8 5.5 %last_terms.1 = (bf16[768,2048]{1,0:T(8,128)(2,1)}, bf16[768,2048]{1,0:T(8,128)(2,1)}, bf16[768,2048]{1,0:T(8,128)(2,1)}, bf16[768,2048]{1,0:T(8,128)(2,1)}) custom-call(bf16[16,768,128]{2,1,0:T(8,128)(2,1)S(1)} %get-tuple-element.18.k, bf16[16,768,128]{2,1,0:T(8,128)(2,1)S(1)} %get-tuple-element.19.v, bf16[16,768,128]{2,1,0:T(8,128)(2,1)S(1)} %get-tuple-element.20.gq, ...), custom_call_target="tpu_custom_call" | custom-call | tf_op jit(solution)/shard_map/last_terms/pallas_call | solution.py:455
  92.3 0.0 copy-done
  92.3 0.6 copy.12
Async XLA Ops:
  86.8 5.5 %copy-start = (f32[16,128]{1,0:T(8,128)S(1)}, f32[16,128]{1,0:T(8,128)}, u32[]{:S(2)}) copy-start(f32[16,128]{1,0:T(8,128)} %get-tuple-element.30) | copy-start | bytes 24580
where the time goes:
time: 93.1 us; the launch traced here: 92.9 us
  Pallas kernels  91.7 us (98%)
    pallas_call x1, Pallas kernels, on_device(): pl.pallas_call(functools.partial(main_kernel, n, peers, chunk), out_shape...  86.2 us
    pallas_call x1, Pallas kernels, on_device(): pl.pallas_call(functools.partial(last_kernel, chunk), out_shape=(rows,) *...  5.48 us

commit v1 on v0

v1 whole, which is shorter than its diff:
```python
import functools

import jax
import jax.numpy as jnp
from jax import lax
from jax.experimental import pallas as pl
from jax.experimental.pallas import tpu as pltpu
from jax.sharding import PartitionSpec as P

DH = 128
EPSILON = 1e-06
CHUNK = 128
F32 = jnp.float32
BF16 = jnp.bfloat16
MESH = pl.DeviceIdType.MESH
HIGHEST = lax.Precision.HIGHEST

AB = ((1,), (0,))
ABT = ((1,), (1,))
ATB = ((0,), (0,))
E_MID, E_TOTAL, E_BEFORE, E_AFTER = range(4)


def mm(left, right, dims):
    return lax.dot_general(left, right, (dims, ((), ())), preferred_element_type=F32)


def exact(left, right, dims):
    return lax.dot_general(left, right, (dims, ((), ())), precision=HIGHEST, preferred_element_type=F32)


def remote(src, dst, send, recv, axis, target):
    return pltpu.make_async_remote_copy(
        src_ref=src, dst_ref=dst, send_sem=send, recv_sem=recv,
        device_id={axis: target}, device_id_type=MESH,
    )


def loop(count, body):
    lax.fori_loop(0, count, lambda i, c: (body(i), c)[1], 0)


def spans(tokens):
    return [slice(j * CHUNK, (j + 1) * CHUNK) for j in range(tokens // CHUNK)]


def causal(x):
    t = lax.broadcasted_iota(jnp.int32, x.shape, 0)
    s = lax.broadcasted_iota(jnp.int32, x.shape, 1)
    return jnp.where(t >= s, x, 0.0).astype(BF16)


def three_terms(x):
    high = x.astype(BF16).astype(F32)
    middle = (x - high).astype(BF16).astype(F32)
    return [high, middle, x - high - middle]


def decay_tables(ld_ref, columns, rows, whole):
    heads, tokens = ld_ref.shape
    below = lax.broadcasted_iota(jnp.int32, (CHUNK, CHUNK), 0)
    right = lax.broadcasted_iota(jnp.int32, (CHUNK, CHUNK), 1)
    tri = (below <= right).astype(F32)
    totals = []
    for j, span in enumerate(spans(tokens)):
        cum = exact(ld_ref[:, span], tri, AB)
        total = jnp.broadcast_to(cum[:, CHUNK - 1 : CHUNK], (heads, DH))
        middle = 0.5 * total
        parts = three_terms(jnp.exp(cum - middle)) + three_terms(jnp.exp(middle - cum))
        rest = columns.shape[1] - 6 * heads
        if rest:
            parts.append(jnp.zeros((rest, CHUNK), F32))
        columns[span] = jnp.concatenate(parts, axis=0).T.astype(BF16)
        rows[E_MID, j] = jnp.exp(middle)
        rows[E_TOTAL, j] = jnp.exp(total)
        totals.append(total)
    count = len(totals)
    run = jnp.zeros((heads, DH), F32)
    for j in range(count):
        rows[E_BEFORE, j] = jnp.exp(run + 0.5 * totals[j])
        run = run + totals[j]
    whole[...] = jnp.exp(run)
    run = jnp.zeros((heads, DH), F32)
    for j in reversed(range(count)):
        rows[E_AFTER, j] = jnp.exp(run + 0.5 * totals[j])
        run = run + totals[j]


def selector(columns, heads, h, first):
    r = lax.broadcasted_iota(jnp.int32, (columns.shape[1], DH), 0) - h - first * heads
    return jnp.where((r == 0) | (r == heads) | (r == 2 * heads), 1.0, 0.0).astype(BF16)


class Chain:
    def __init__(self, n, index, reverse, whole, partner_whole, bufs, recv_sems, send_sems):
        (self.lsend, self.lrecv, self.zsend, self.zrecv, self.xsend, self.xrecv) = bufs
        self.recv_sems, self.send_sems, self.index = recv_sems, send_sems, index
        self.whole, self.partner_whole = whole, partner_whole
        me = lax.axis_index("seq")
        self.partner = me + 1 - 2 * lax.rem(me, 2)
        place = n - 1 - me if reverse else me
        self.later = lax.rem(place, 2)
        self.row = place // 2
        self.first = self.row == 0
        self.last = self.row == n // 2 - 1
        step = -2 if reverse else 2
        self.next = lax.rem(me + step + n, n)

    def led(self, s):
        return 2 * s + 1 - self.later

    def other(self, s):
        return 2 * s + self.later

    def copy(self, kind, src, dst, h, target):
        return remote(src, dst, self.send_sems.at[self.index, kind], self.recv_sems.at[kind, h], "seq", target)

    def copy_l(self, h):
        return self.copy(0, self.lsend.at[h], self.lrecv.at[h], h, self.partner)

    def copy_x(self, h):
        return self.copy(1, self.xsend.at[h], self.xrecv.at[h], h, self.partner)

    def copy_z(self, h):
        return self.copy(2, self.zsend.at[h], self.zrecv.at[h], h, self.next)

    def start(self):
        @pl.when(self.first)
        def _():
            self.zrecv[...] = jnp.zeros_like(self.zrecv)

    def step(self, h, take):
        self.copy_l(h).wait_recv()

        @pl.when(jnp.logical_not(self.first))
        def _():
            self.copy_z(h).wait_recv()

        state = self.zrecv[h]
        own, theirs = self.whole[pl.ds(h, 1), :], self.partner_whole[pl.ds(h, 1), :]

        @pl.when(self.later == 1)
        def _():
            mid = theirs * state + self.lrecv[h]
            self.zsend[h] = own * mid + self.lsend[h]
            self.xsend[h] = state
            take(h, mid)

        @pl.when(self.later == 0)
        def _():
            mid = own * state + self.lsend[h]
            self.zsend[h] = theirs * mid + self.lrecv[h]
            self.xsend[h] = mid
            take(h, state)

        @pl.when(jnp.logical_not(self.last))
        def _():
            self.copy_z(h).start()

        self.copy_x(h).start()

    def take(self, h, take):
        self.copy_x(h).wait_recv()
        take(h, self.xrecv[h])

    def wait_l(self, half):
        self.copy(0, self.lsend.at[0:half], self.lrecv.at[0:half], 0, self.partner).wait_send()

    def wait_xz(self, half):
        self.copy(1, self.xsend.at[0:half], self.xrecv.at[0:half], 0, self.partner).wait_send()

        @pl.when(jnp.logical_not(self.last))
        def _():
            self.copy(2, self.zsend.at[0:half], self.zrecv.at[0:half], 0, self.next).wait_send()


def main_kernel(
    n, peers,
    q_hbm, k_hbm, v_hbm, g_hbm, ld_ref, gain_ref,
    q, k, kd, g, att, obuf, r_out, rows, gg_out,
    v, qd, ga, wt, qs, ts, columns, state_in, sq_acc, in_acc, inv_b, cen_b,
    whole, partner_whole,
    stat_send, stat_recv, gain_send, gain_recv,
    lsend, lrecv, zsend, zrecv, xsend, xrecv,
    load_sem, g_sem, recv_sems, send_sems, pair_sem, stat_sem, gain_sem,
):
    heads, tokens, _ = q.shape
    half = heads // 2
    parts = list(enumerate(spans(tokens)))
    final = len(parts) - 1
    me = lax.axis_index("seq")
    my_head = lax.axis_index("head")
    width = heads * DH * peers

    barrier = pltpu.get_barrier_semaphore()
    for off in range(1, n):
        pl.semaphore_signal(barrier, inc=1, device_id={"seq": lax.rem(me + off, n)}, device_id_type=MESH)
    for off in range(1, peers):
        pl.semaphore_signal(barrier, inc=1, device_id={"head": lax.rem(my_head + off, peers)}, device_id_type=MESH)

    def load(hbm, vmem, h, sem):
        where = pl.ds(pl.multiple_of(h * DH, DH), DH)
        pltpu.make_async_copy(hbm.at[:, where], vmem.at[h], sem).start()

    def landed(vmem, count, sem):
        pltpu.make_async_copy(vmem.at[0:count], vmem.at[0:count], sem).wait()

    def load_kv(p):
        for h in (2 * p, 2 * p + 1):
            load(k_hbm, k, h, load_sem.at[0, p])
            load(v_hbm, v, h, load_sem.at[0, p])

    def load_q(p):
        for h in (2 * p, 2 * p + 1):
            load(q_hbm, q, h, load_sem.at[1, p])

    def load_g(p):
        for h in (2 * p, 2 * p + 1):
            load(g_hbm, g, h, g_sem)

    loop(half, load_kv)
    loop(half, load_q)
    loop(half, load_g)
    decay_tables(ld_ref, columns, rows, whole)
    bufs = (lsend, lrecv, zsend, zrecv, xsend, xrecv)
    forward = Chain(n, 0, False, whole, partner_whole, bufs, recv_sems, send_sems)
    backward = Chain(n, 1, True, whole, partner_whole, bufs, recv_sems, send_sems)
    forward.start()

    def row(kind, j, h):
        return rows[kind, j, pl.ds(h, 1), :]

    def local_pair(p):
        landed(k, 4, load_sem.at[0, p])
        keys = {}
        for i, h in enumerate((2 * p, 2 * p + 1)):
            pick = selector(columns, heads, h, 3)
            for j, span in parts:
                keys[i, j] = (k[h, span].astype(F32) * mm(columns[span], pick, AB)).astype(BF16)
                kd[h, span] = keys[i, j]
        for i, h in enumerate((2 * p, 2 * p + 1)):
            state = None
            for j, span in parts:
                part = row(E_MID, j, h) * mm(keys[i, j], v[h, span], ATB)
                if j:
                    qs[h, j] = (row(E_MID, j, h) * state).astype(BF16)
                state = part if j == 0 else row(E_TOTAL, j, h) * state + part
            lsend[h] = state

    def pair_copy():
        return remote(whole, partner_whole, pair_sem.at[0], pair_sem.at[1], "seq", forward.partner)

    local_pair(0)
    pl.semaphore_wait(barrier, n - 1 + peers - 1)
    pair_copy().start()
    forward.copy_l(forward.other(0)).start()

    def local_rest(i):
        local_pair(i + 1)
        forward.copy_l(forward.other(i + 1)).start()

    loop(half - 1, local_rest)

    def intra_pair(p):
        landed(q, 2, load_sem.at[1, p])
        queries, weights = {}, {}
        both = [(i, j, 2 * p + i, span) for i in (0, 1) for j, span in parts]
        picks = [selector(columns, heads, 2 * p + i, 0) for i in (0, 1)]
        for i, j, h, span in both:
            queries[i, j] = (q[h, span].astype(F32) * mm(columns[span], picks[i], AB)).astype(BF16)
            qd[h, span] = queries[i, j]
        for i, j, h, span in both:
            weights[i, j] = causal(mm(queries[i, j], kd[h, span], ABT))
            wt[h, span] = weights[i, j].T
        for i, j, h, span in both:
            if j:
                left = jnp.concatenate([weights[i, j], queries[i, j]], axis=1)
                right = jnp.concatenate([v[h, span], qs[h, j]], axis=0)
                att[h, span] = mm(left, right, AB)
            else:
                att[h, span] = mm(weights[i, j], v[h, span], AB)

    def arrive(h):
        state = state_in[h].astype(BF16)
        gain = gain_ref[pl.ds(h, 1), :]
        for j, span in parts:
            value = att[h, span] + row(E_BEFORE, j, h) * mm(qd[h, span], state, AB)
            att[h, span] = value
            sq_acc[span] += value * value
            in_acc[span] += g[h, span].astype(F32) * gain * value

    def keep_in(h, state):
        state_in[h] = state

    sq_acc[...] = jnp.zeros_like(sq_acc)
    in_acc[...] = jnp.zeros_like(in_acc)
    pair_copy().wait_recv()
    landed(g, heads, g_sem)
    lag = jnp.minimum(4 * forward.row, half)

    def forward_turn(i):
        at = i - lag
        ready = jnp.logical_and(at >= 0, at < half)

        @pl.when(ready)
        def _():
            forward.step(forward.led(at), keep_in)

        @pl.when(i < half)
        def _():
            intra_pair(i)

        @pl.when(ready)
        def _():
            arrive(forward.led(at))

    loop(half + lag, forward_turn)

    def forward_take(s):
        forward.take(forward.other(s), keep_in)
        arrive(forward.other(s))

    loop(half, forward_take)

    count = len(parts)
    lane = lax.broadcasted_iota(jnp.int32, (CHUNK, DH), 1)
    sums = jnp.zeros((CHUNK, DH), F32)
    for j, span in parts:
        sums = jnp.where(lane == j, jnp.sum(sq_acc[span], axis=1, keepdims=True), sums)
        sums = jnp.where(lane == count + j, jnp.sum(in_acc[span], axis=1, keepdims=True), sums)
    stat_send[...] = sums.T[0 : stat_send.shape[0]]

    def stat_copy(off):
        return remote(
            stat_send, stat_recv.at[my_head], stat_sem.at[0], stat_sem.at[1],
            "head", lax.rem(my_head + off, peers),
        )

    for off in range(1, peers):
        stat_copy(off).start()
    stat_recv[my_head] = stat_send[...]
    forward.wait_l(half)
    backward.start()
    many = stat_recv.at[0 : peers - 1]
    remote(many, many, stat_sem.at[0], stat_sem.at[1], "head", lax.rem(my_head + 1, peers)).wait_recv()
    stats = stat_recv[0]
    for i in range(1, peers):
        stats = stats + stat_recv[i]
    inverse = lax.rsqrt(stats[0:count] / width + EPSILON)
    center = stats[count : 2 * count] * inverse / width
    terms = three_terms(jnp.concatenate([inverse, center], axis=0))
    scales = jnp.concatenate(terms + [jnp.zeros((DH - 6 * count, DH), F32)], axis=0).T.astype(BF16)
    r = lax.broadcasted_iota(jnp.int32, (DH, 2 * DH), 0)
    base = jnp.where(lax.broadcasted_iota(jnp.int32, (DH, 2 * DH), 1) < DH, r, r - count)
    for j, span in parts:
        hit = (base == j) | (base == 2 * count + j) | (base == 4 * count + j)
        wide = mm(scales, jnp.where(hit, 1.0, 0.0).astype(BF16), AB)
        inv_b[span] = wide[:, :DH]
        cen_b[span] = wide[:, DH:]

    def normalize(h):
        gain = gain_ref[pl.ds(h, 1), :]
        gain_part = jnp.zeros((8, DH), F32)
        state = None
        for j, span in reversed(parts):
            scale = inv_b[span]
            normed = att[h, span] * scale
            obuf[h, span] = (normed * gain).astype(BF16)
            cotangent = g[h, span].astype(F32)
            gain_part = gain_part + jnp.sum((cotangent * normed).reshape(CHUNK // 8, 8, DH), axis=0)
            grad = (scale * (cotangent * gain - normed * cen_b[span])).astype(BF16)
            ga[h, span] = grad
            part = row(E_MID, j, h) * mm(qd[h, span], grad, ATB)
            if j < final:
                ts[h, j] = (row(E_MID, j, h) * state).astype(BF16)
            state = part if j == final else row(E_TOTAL, j, h) * state + part
        lsend[h] = state
        gain_send[pl.ds(h, 1), :] = jnp.sum(gain_part, axis=0, keepdims=True)

    def gradients(h):
        incoming = state_in[h]
        pick = jnp.concatenate([selector(columns, heads, h, 0), selector(columns, heads, h, 3)], axis=1)
        grad_weights, inter, scale = {}, {}, {}
        for j, span in parts:
            before = row(E_BEFORE, j, h) * incoming
            if j:
                before = before + qs[h, j].astype(F32)
            both = mm(ga[h, span], jnp.concatenate([v[h, span], before.astype(BF16)], axis=0), ABT)
            grad_weights[j], inter[j] = causal(both[:, :CHUNK]), both[:, CHUNK:]
        for j, span in parts:
            scale[j] = mm(columns[span], pick, AB)
            g[h, span] = (scale[j][:, DH:] * v[h, span].astype(F32)).astype(BF16)
        for j, span in parts:
            grad_q = mm(grad_weights[j], kd[h, span], AB) + inter[j]
            k[h, span] = (scale[j][:, :DH] * grad_q).astype(BF16)
        for j, span in parts:
            left, right = grad_weights[j].T, qd[h, span]
            if j < final:
                left = jnp.concatenate([left, v[h, span]], axis=1)
                right = jnp.concatenate([right, ts[h, j].T], axis=0)
            att[h, span] = scale[j][:, DH:] * mm(left, right, AB)
        for j, span in parts:
            left, right = wt[h, span], ga[h, span]
            if j < final:
                left = jnp.concatenate([left, kd[h, span]], axis=1)
                right = jnp.concatenate([right, ts[h, j]], axis=0)
            q[h, span] = mm(left, right, AB).astype(BF16)

    def keep_out(h, state):
        r_out[h] = state.astype(BF16)

    def gain_copy(off):
        return remote(
            gain_send, gain_recv.at[me], gain_sem.at[0], gain_sem.at[1], "seq", lax.rem(me + off, n),
        )

    def normalize_pair(i):
        normalize(2 * i)
        normalize(2 * i + 1)
        backward.copy_l(backward.other(i)).start()

    loop(half, normalize_pair)
    for off in range(1, n):
        gain_copy(off).start()
    back_lag = jnp.maximum(3 * backward.row - 1, 0)

    def backward_turn(i):
        at = i - back_lag

        @pl.when(jnp.logical_and(at >= 0, at < half))
        def _():
            backward.step(backward.led(at), keep_out)

        @pl.when(i < half)
        def _():
            loop(2, lambda o: gradients(2 * i + o))

    loop(half + back_lag, backward_turn)

    def backward_take(s):
        backward.take(backward.other(s), keep_out)

    loop(half, backward_take)

    gain_recv[me] = gain_send[...]
    many_gains = gain_recv.at[0 : n - 1]
    remote(many_gains, many_gains, gain_sem.at[0], gain_sem.at[1], "seq", forward.partner).wait_recv()
    gain_total = gain_recv[0]
    for i in range(1, n):
        gain_total = gain_total + gain_recv[i]
    gg_out[...] = gain_total

    pair_copy().wait_send()
    forward.wait_xz(half)
    backward.wait_l(half)
    backward.wait_xz(half)
    remote(many, many, stat_sem.at[0], stat_sem.at[1], "head", lax.rem(my_head + 1, peers)).wait_send()
    remote(many_gains, many_gains, gain_sem.at[0], gain_sem.at[1], "seq", forward.partner).wait_send()


def last_kernel(
    gv, gq, kd, vk, gk, out, after, rows, gg,
    out_hbm, gq_hbm, gk_hbm, gv_hbm, gg_hbm, k_stage, v_stage, store_sem,
):
    heads, tokens, _ = kd.shape

    def store(i, vmem, hbm, h):
        where = pl.ds(pl.multiple_of(h * DH, DH), DH)
        pltpu.make_async_copy(vmem.at[h], hbm.at[:, where], store_sem.at[i]).start()

    gains = pltpu.make_async_copy(gg, gg_hbm, store_sem.at[4])
    gains.start()

    def final_terms(h):
        state = after[h]
        for j, span in enumerate(spans(tokens)):
            decay = rows[E_AFTER, j, pl.ds(h, 1), :]
            k_stage[h, span] = (gk[h, span] + decay * mm(vk[h, span], state, ABT)).astype(BF16)
            v_stage[h, span] = (gv[h, span].astype(F32) + decay * mm(kd[h, span], state, AB)).astype(BF16)

    def two(p):
        for h in (2 * p, 2 * p + 1):
            store(0, out, out_hbm, h)
            store(1, gq, gq_hbm, h)
        for h in (2 * p, 2 * p + 1):
            final_terms(h)
        for h in (2 * p, 2 * p + 1):
            store(2, k_stage, gk_hbm, h)
            store(3, v_stage, gv_hbm, h)

    loop(heads // 2, two)
    for i in range(4):
        pltpu.make_async_copy(k_stage, k_stage, store_sem.at[i]).wait()
    gains.wait()


def on_device(n, peers, queries, key_rows, value_rows, log_decay, norm_gain, grad_out):
    tokens, width = queries.shape
    heads = width // DH
    chunks = tokens // CHUNK
    depth = -(-6 * heads // DH) * DH
    gain = norm_gain.reshape(heads, DH)
    anywhere = pl.BlockSpec(memory_space=pl.ANY)
    vmem = pl.BlockSpec(memory_space=pltpu.VMEM)
    rows = jax.ShapeDtypeStruct((tokens, width), BF16)
    gains = jax.ShapeDtypeStruct((heads, DH), F32)
    per_head = lambda *shape, dtype=F32: pltpu.VMEM((heads, *shape), dtype)
    dma = pltpu.SemaphoreType.DMA
    by_head = lambda dtype: pltpu.VMEM((heads, tokens, DH), dtype)
    states = pltpu.VMEM((heads, chunks, DH, DH), BF16)
    flat = pltpu.VMEM((tokens, DH), F32)
    stat_rows = -(-2 * chunks // 8) * 8
    q, k, kd, g, att, out, after, table, grad_gain = pl.pallas_call(
        functools.partial(main_kernel, n, peers),
        out_shape=(
            by_head(BF16), by_head(BF16), by_head(BF16), by_head(BF16), by_head(F32), by_head(BF16),
            pltpu.VMEM((heads, DH, DH), BF16),
            pltpu.VMEM((4, chunks, heads, DH), F32), pltpu.VMEM((heads, DH), F32),
        ),
        in_specs=[anywhere] * 4 + [vmem] * 2,
        out_specs=(vmem,) * 9,
        scratch_shapes=[
            *[by_head(BF16)] * 4, states, states, pltpu.VMEM((tokens, depth), BF16),
            per_head(DH, DH), flat, flat, flat, flat,
            pltpu.VMEM((heads, DH), F32), pltpu.VMEM((heads, DH), F32),
            pltpu.VMEM((stat_rows, DH), F32), pltpu.VMEM((peers, stat_rows, DH), F32),
            pltpu.VMEM((heads, DH), F32), pltpu.VMEM((n, heads, DH), F32),
            *[per_head(DH, DH)] * 6,
            dma((2, heads // 2)), dma, dma((3, heads)), dma((2, 3)), dma((2,)), dma((2,)), dma((2,)),
        ],
        compiler_params=pltpu.CompilerParams(
            collective_id=0, has_side_effects=True, vmem_limit_bytes=36 * 1024 * 1024
        ),
        name="forward_chain",
    )(queries, key_rows, value_rows, grad_out, log_decay, gain)
    out, grad_q, grad_k, grad_v, grad_gain = pl.pallas_call(
        last_kernel,
        out_shape=(rows,) * 4 + (gains,),
        in_specs=[vmem] * 9,
        out_specs=(anywhere,) * 5,
        scratch_shapes=[by_head(BF16), by_head(BF16), dma((5,))],
        compiler_params=pltpu.CompilerParams(vmem_limit_bytes=16 * 1024 * 1024),
        name="last_terms",
    )(q, k, kd, g, att, out, after, table, grad_gain)
    return out, grad_q, grad_k, grad_v, grad_gain.reshape(width)


def solution(mesh):
    in_specs = (
        P("seq", "head"),
        P("seq", "head"),
        P("seq", "head"),
        P("head", "seq"),
        P("head"),
        P("seq", "head"),
    )
    out_specs = (P("seq", "head"), P("seq", "head"), P("seq", "head"), P("seq", "head"), P("head"))
    return jax.shard_map(
        functools.partial(on_device, mesh.shape["seq"], mesh.shape["head"]),
        mesh=mesh, in_specs=in_specs, out_specs=out_specs, check_vma=False,
    )
```

time: 93.1 us -> 72.5 us (0.78)
  Pallas kernels: 91.7 us -> 71.7 us
    pallas_call x2, Pallas kernels: 91.7 us -> 71.7 us  [the longest x1 66.8 us: on_device(): pl.pallas_call(functools.partial(main_kernel, n, peers), out_shape=(by_he...]
where the time goes in v1:
time: 72.5 us; the launch traced here: 72.3 us
  Pallas kernels  71.7 us (99%)
    pallas_call x1, Pallas kernels, on_device(): pl.pallas_call(functools.partial(main_kernel, n, peers), out_shape=(by_he...  66.8 us
    pallas_call x1, Pallas kernels, on_device(): pl.pallas_call(last_kernel, out_shape=(rows,) * 4 + (gains,), in_specs=[v...  4.9 us

profile of v1, /device:TPU:0, one launch (start us, length us, event | category | flops | bytes accessed | tf_op | source)
XLA Modules:
  0.0 72.3 jit_solution(17217397316605818273)
XLA Ops:
  0.6 66.8 %forward_chain.1 = (bf16[16,768,128]{2,1,0:T(8,128)(2,1)S(1)}, bf16[16,768,128]{2,1,0:T(8,128)(2,1)S(1)}, bf16[16,768,128]{2,1,0:T(8,128)(2,1)S(1)}, bf16[16,768...) custom-call(bf16[768,2048]{1,0:T(8,128)(2,1)} %q_hbm.1, ...), custom_call_target="tpu_custom_call" | custom-call | tf_op jit(solution)/shard_map/forward_chain/pallas_call | solution.py:513
  67.4 4.9 %last_terms.1 = (bf16[768,2048]{1,0:T(8,128)(2,1)}, bf16[768,2048]{1,0:T(8,128)(2,1)}, bf16[768,2048]{1,0:T(8,128)(2,1)}, bf16[768,2048]{1,0:T(8,128)(2,1)}, f32[16,128]{1,0:T(8,128)}) custom-call(bf16[16,768,128]{2,1,0:T(8,128)(2,1)S(1)} %get-tuple-element.19.gv, bf16[16,768,128]{2,1,0:T(8,128)(2,1)S(1)} %get-tuple-element.20.gq, ...), custom_call_target="tpu_custom_call" | custom-call | tf_op jit(solution)/shard_map/last_terms/pallas_call | solution.py:536

commit v2 on v1

--- a/solution.py
+++ b/solution.py
@@ -19,6 +19,7 @@
 ABT = ((1,), (1,))
 ATB = ((0,), (0,))
 E_MID, E_TOTAL, E_BEFORE, E_AFTER = range(4)
+PIECES = (slice(0, DH // 2), slice(DH // 2, DH))
 
 
 def mm(left, right, dims):
@@ -56,24 +57,30 @@
     return [high, middle, x - high - middle]
 
 
-def decay_tables(ld_ref, columns, rows, whole):
-    heads, tokens = ld_ref.shape
+def decay_tables(ld, columns, rows, whole):
+    heads, tokens = ld.shape
     below = lax.broadcasted_iota(jnp.int32, (CHUNK, CHUNK), 0)
     right = lax.broadcasted_iota(jnp.int32, (CHUNK, CHUNK), 1)
-    tri = (below <= right).astype(F32)
+    tri = (below <= right).astype(F32).astype(BF16)
+    parts = spans(tokens)
+    stacked = jnp.concatenate([ld[:, span] for span in parts], axis=0)
+    left = jnp.concatenate([x.astype(BF16) for x in three_terms(stacked)], axis=1)
+    cum = mm(left, jnp.concatenate([tri] * 3, axis=0), AB)
+    total = jnp.broadcast_to(cum[:, CHUNK - 1 : CHUNK], cum.shape)
+    middle = 0.5 * total
+    terms = three_terms(jnp.exp(cum - middle)) + three_terms(jnp.exp(middle - cum))
+    exp_middle, exp_total = jnp.exp(middle), jnp.exp(total)
+    rest = columns.shape[1] - 6 * heads
     totals = []
-    for j, span in enumerate(spans(tokens)):
-        cum = exact(ld_ref[:, span], tri, AB)
-        total = jnp.broadcast_to(cum[:, CHUNK - 1 : CHUNK], (heads, DH))
-        middle = 0.5 * total
-        parts = three_terms(jnp.exp(cum - middle)) + three_terms(jnp.exp(middle - cum))
-        rest = columns.shape[1] - 6 * heads
+    for j, span in enumerate(parts):
+        own = slice(j * heads, (j + 1) * heads)
+        stack = [x[own] for x in terms]
         if rest:
-            parts.append(jnp.zeros((rest, CHUNK), F32))
-        columns[span] = jnp.concatenate(parts, axis=0).T.astype(BF16)
-        rows[E_MID, j] = jnp.exp(middle)
-        rows[E_TOTAL, j] = jnp.exp(total)
-        totals.append(total)
+            stack.append(jnp.zeros((rest, CHUNK), F32))
+        columns[span] = jnp.concatenate(stack, axis=0).T.astype(BF16)
+        rows[E_MID, j] = exp_middle[own]
+        rows[E_TOTAL, j] = exp_total[own]
+        totals.append(total[own])
     count = len(totals)
     run = jnp.zeros((heads, DH), F32)
     for j in range(count):
@@ -92,9 +99,9 @@
 
 
 class Chain:
-    def __init__(self, n, index, reverse, whole, partner_whole, bufs, recv_sems, send_sems):
+    def __init__(self, n, reverse, whole, partner_whole, bufs, recv_sems, x_sems, send_sems):
         (self.lsend, self.lrecv, self.zsend, self.zrecv, self.xsend, self.xrecv) = bufs
-        self.recv_sems, self.send_sems, self.index = recv_sems, send_sems, index
+        self.recv_sems, self.x_sems, self.send_sems = recv_sems, x_sems, send_sems
         self.whole, self.partner_whole = whole, partner_whole
         me = lax.axis_index("seq")
         self.partner = me + 1 - 2 * lax.rem(me, 2)
@@ -112,77 +119,83 @@
     def other(self, s):
         return 2 * s + self.later
 
-    def copy(self, kind, src, dst, h, target):
-        return remote(src, dst, self.send_sems.at[self.index, kind], self.recv_sems.at[kind, h], "seq", target)
-
-    def copy_l(self, h):
-        return self.copy(0, self.lsend.at[h], self.lrecv.at[h], h, self.partner)
-
-    def copy_x(self, h):
-        return self.copy(1, self.xsend.at[h], self.xrecv.at[h], h, self.partner)
-
-    def copy_z(self, h):
-        return self.copy(2, self.zsend.at[h], self.zrecv.at[h], h, self.next)
+    def copy(self, kind, src, dst, s, i, target):
+        return remote(src, dst, self.send_sems.at[2 * kind], self.recv_sems.at[kind, s, i], "seq", target)
+
+    def copy_l(self, s, i):
+        src = self.lsend.at[self.other(s), PIECES[i]]
+        return self.copy(0, src, self.lrecv.at[s, PIECES[i]], s, i, self.partner)
+
+    def copy_x(self, s):
+        return remote(self.xsend.at[s], self.xrecv.at[s], self.send_sems.at[1], self.x_sems.at[s], "seq", self.partner)
+
+    def copy_z(self, s, i):
+        return self.copy(1, self.zsend.at[s, PIECES[i]], self.zrecv.at[s, PIECES[i]], s, i, self.next)
 
     def start(self):
         @pl.when(self.first)
         def _():
             self.zrecv[...] = jnp.zeros_like(self.zrecv)
 
-    def step(self, h, take):
-        self.copy_l(h).wait_recv()
-
-        @pl.when(jnp.logical_not(self.first))
-        def _():
-            self.copy_z(h).wait_recv()
-
-        state = self.zrecv[h]
+    def give(self, s):
+        for i in range(len(PIECES)):
+            self.copy_l(s, i).start()
+
+    def step(self, s, take):
+        h = self.led(s)
         own, theirs = self.whole[pl.ds(h, 1), :], self.partner_whole[pl.ds(h, 1), :]
-
-        @pl.when(self.later == 1)
-        def _():
-            mid = theirs * state + self.lrecv[h]
-            self.zsend[h] = own * mid + self.lsend[h]
-            self.xsend[h] = state
-            take(h, mid)
-
-        @pl.when(self.later == 0)
-        def _():
-            mid = own * state + self.lsend[h]
-            self.zsend[h] = theirs * mid + self.lrecv[h]
-            self.xsend[h] = mid
-            take(h, state)
+        for i, piece in enumerate(PIECES):
+            @pl.when(jnp.logical_not(self.first))
+            def _():
+                self.copy_z(s, i).wait_recv()
+
+            self.copy_l(s, i).wait_recv()
+            state, mine, other = self.zrecv[s, piece], self.lsend[h, piece], self.lrecv[s, piece]
+
+            @pl.when(self.later == 1)
+            def _():
+                mid = theirs * state + other
+                self.zsend[s, piece] = own * mid + mine
+                self.xsend[s, piece] = state
+                take(h, piece, mid)
+
+            @pl.when(self.later == 0)
+            def _():
+                mid = own * state + mine
+                self.zsend[s, piece] = theirs * mid + other
+                self.xsend[s, piece] = mid
+                take(h, piece, state)
+
+            @pl.when(jnp.logical_not(self.last))
+            def _():
+                self.copy_z(s, i).start()
+
+        self.copy_x(s).start()
+
+    def take(self, s, take):
+        self.copy_x(s).wait_recv()
+        take(self.other(s), slice(0, DH), self.xrecv[s])
+
+    def sent(self):
+        half = self.xsend.shape[0]
+        mine = self.lsend.at[0:half]
+        self.copy(0, mine, self.lrecv, 0, 0, self.partner).wait_send()
+        remote(self.xsend, self.xrecv, self.send_sems.at[1], self.x_sems.at[0], "seq", self.partner).wait_send()
 
         @pl.when(jnp.logical_not(self.last))
         def _():
-            self.copy_z(h).start()
-
-        self.copy_x(h).start()
-
-    def take(self, h, take):
-        self.copy_x(h).wait_recv()
-        take(h, self.xrecv[h])
-
-    def wait_l(self, half):
-        self.copy(0, self.lsend.at[0:half], self.lrecv.at[0:half], 0, self.partner).wait_send()
-
-    def wait_xz(self, half):
-        self.copy(1, self.xsend.at[0:half], self.xrecv.at[0:half], 0, self.partner).wait_send()
-
-        @pl.when(jnp.logical_not(self.last))
-        def _():
-            self.copy(2, self.zsend.at[0:half], self.zrecv.at[0:half], 0, self.next).wait_send()
+            self.copy(1, self.zsend, self.zrecv, 0, 0, self.next).wait_send()
 
 
 def main_kernel(
     n, peers,
-    q_hbm, k_hbm, v_hbm, g_hbm, ld_ref, gain_ref,
+    q_hbm, k_hbm, v_hbm, g_hbm, ld_hbm, gain_hbm,
     q, k, kd, g, att, obuf, r_out, rows, gg_out,
-    v, qd, ga, wt, qs, ts, columns, state_in, sq_acc, in_acc, inv_b, cen_b,
+    v, qd, ga, wt, qs, ts, columns, ld, gain_ref, state_in, sq_acc, in_acc, inv_b, cen_b,
     whole, partner_whole,
     stat_send, stat_recv, gain_send, gain_recv,
     lsend, lrecv, zsend, zrecv, xsend, xrecv,
-    load_sem, g_sem, recv_sems, send_sems, pair_sem, stat_sem, gain_sem,
+    once_sem, recv_sems, x_sems, send_sems, pair_sem, stat_sem, gain_sem, tokens_sem,
 ):
     heads, tokens, _ = q.shape
     half = heads // 2
@@ -192,12 +205,6 @@
     my_head = lax.axis_index("head")
     width = heads * DH * peers
 
-    barrier = pltpu.get_barrier_semaphore()
-    for off in range(1, n):
-        pl.semaphore_signal(barrier, inc=1, device_id={"seq": lax.rem(me + off, n)}, device_id_type=MESH)
-    for off in range(1, peers):
-        pl.semaphore_signal(barrier, inc=1, device_id={"head": lax.rem(my_head + off, peers)}, device_id_type=MESH)
-
     def load(hbm, vmem, h, sem):
         where = pl.ds(pl.multiple_of(h * DH, DH), DH)
         pltpu.make_async_copy(hbm.at[:, where], vmem.at[h], sem).start()
@@ -205,40 +212,59 @@
     def landed(vmem, count, sem):
         pltpu.make_async_copy(vmem.at[0:count], vmem.at[0:count], sem).wait()
 
-    def load_kv(p):
+    def landed_twice(count, sem):
+        pltpu.make_async_copy(att.at[0:count], att.at[0:count], sem).wait()
+
+    def load_kv(p, sem):
         for h in (2 * p, 2 * p + 1):
-            load(k_hbm, k, h, load_sem.at[0, p])
-            load(v_hbm, v, h, load_sem.at[0, p])
+            load(k_hbm, k, h, sem)
+            load(v_hbm, v, h, sem)
 
     def load_q(p):
         for h in (2 * p, 2 * p + 1):
-            load(q_hbm, q, h, load_sem.at[1, p])
+            load(q_hbm, q, h, once_sem.at[3])
 
     def load_g(p):
         for h in (2 * p, 2 * p + 1):
-            load(g_hbm, g, h, g_sem)
-
-    loop(half, load_kv)
+            load(g_hbm, g, h, once_sem.at[0])
+
+    ld_copy = pltpu.make_async_copy(ld_hbm, ld, once_sem.at[1])
+    gain_in = pltpu.make_async_copy(gain_hbm, gain_ref, once_sem.at[2])
+    ld_copy.start()
+    load_kv(0, once_sem.at[4])
+    loop(half - 1, lambda p: load_kv(p + 1, once_sem.at[5]))
+    gain_in.start()
+    barrier = pltpu.get_barrier_semaphore()
+    at_start, at_end = me < 2, me >= n - 2
+
+    def signal(semaphore, axis, target):
+        pl.semaphore_signal(semaphore, inc=1, device_id={axis: target}, device_id_type=MESH)
+
+    signal(barrier, "seq", me + 1 - 2 * lax.rem(me, 2))
+    for off in range(1, peers):
+        signal(barrier, "head", lax.rem(my_head + off, peers))
+    pl.when(jnp.logical_not(at_start))(lambda: signal(barrier, "seq", lax.rem(me + n - 2, n)))
+    pl.when(jnp.logical_not(at_end))(lambda: signal(barrier, "seq", lax.rem(me + 2, n)))
     loop(half, load_q)
     loop(half, load_g)
-    decay_tables(ld_ref, columns, rows, whole)
+    ld_copy.wait()
+    decay_tables(ld, columns, rows, whole)
     bufs = (lsend, lrecv, zsend, zrecv, xsend, xrecv)
-    forward = Chain(n, 0, False, whole, partner_whole, bufs, recv_sems, send_sems)
-    backward = Chain(n, 1, True, whole, partner_whole, bufs, recv_sems, send_sems)
+    forward = Chain(n, False, whole, partner_whole, bufs, recv_sems, x_sems, send_sems)
+    backward = Chain(n, True, whole, partner_whole, bufs, recv_sems, x_sems, send_sems)
     forward.start()
 
     def row(kind, j, h):
         return rows[kind, j, pl.ds(h, 1), :]
 
-    def local_pair(p):
-        landed(k, 4, load_sem.at[0, p])
+    def local_states(group):
         keys = {}
-        for i, h in enumerate((2 * p, 2 * p + 1)):
+        for i, h in enumerate(group):
             pick = selector(columns, heads, h, 3)
             for j, span in parts:
                 keys[i, j] = (k[h, span].astype(F32) * mm(columns[span], pick, AB)).astype(BF16)
                 kd[h, span] = keys[i, j]
-        for i, h in enumerate((2 * p, 2 * p + 1)):
+        for i, h in enumerate(group):
             state = None
             for j, span in parts:
                 part = row(E_MID, j, h) * mm(keys[i, j], v[h, span], ATB)
@@ -250,19 +276,31 @@
     def pair_copy():
         return remote(whole, partner_whole, pair_sem.at[0], pair_sem.at[1], "seq", forward.partner)
 
-    local_pair(0)
-    pl.semaphore_wait(barrier, n - 1 + peers - 1)
+    landed(k, 4, once_sem.at[4])
+    local_states([forward.other(0)])
+    neighbours = peers + jnp.where(at_start, 0, 1) + jnp.where(at_end, 0, 1)
+    pl.semaphore_wait(barrier, neighbours)
+    forward.give(0)
     pair_copy().start()
-    forward.copy_l(forward.other(0)).start()
+
+    def pass_up():
+        pl.when(jnp.logical_not(at_end))(lambda: signal(tokens_sem.at[0], "seq", lax.rem(me + 2, n)))
+
+    def pass_down():
+        pl.when(jnp.logical_not(at_start))(lambda: signal(tokens_sem.at[1], "seq", lax.rem(me + n - 2, n)))
+
+    pl.when(at_start)(pass_up)
+    pl.when(at_end)(pass_down)
+    local_states([forward.led(0)])
 
     def local_rest(i):
-        local_pair(i + 1)
-        forward.copy_l(forward.other(i + 1)).start()
-
+        local_states([2 * i + 2, 2 * i + 3])
+        forward.give(i + 1)
+
+    landed_twice(heads - 2, once_sem.at[5])
     loop(half - 1, local_rest)
 
     def intra_pair(p):
-        landed(q, 2, load_sem.at[1, p])
         queries, weights = {}, {}
         both = [(i, j, 2 * p + i, span) for i in (0, 1) for j, span in parts]
         picks = [selector(columns, heads, 2 * p + i, 0) for i in (0, 1)]
@@ -289,13 +327,15 @@
             sq_acc[span] += value * value
             in_acc[span] += g[h, span].astype(F32) * gain * value
 
-    def keep_in(h, state):
-        state_in[h] = state
+    def keep_in(h, piece, state):
+        state_in[h, piece] = state
 
     sq_acc[...] = jnp.zeros_like(sq_acc)
     in_acc[...] = jnp.zeros_like(in_acc)
     pair_copy().wait_recv()
-    landed(g, heads, g_sem)
+    gain_in.wait()
+    landed(q, heads, once_sem.at[3])
+    landed(g, heads, once_sem.at[0])
     lag = jnp.minimum(4 * forward.row, half)
 
     def forward_turn(i):
@@ -304,7 +344,7 @@
 
         @pl.when(ready)
         def _():
-            forward.step(forward.led(at), keep_in)
+            forward.step(at, keep_in)
 
         @pl.when(i < half)
         def _():
@@ -317,7 +357,7 @@
     loop(half + lag, forward_turn)
 
     def forward_take(s):
-        forward.take(forward.other(s), keep_in)
+        forward.take(s, keep_in)
         arrive(forward.other(s))
 
     loop(half, forward_take)
@@ -339,7 +379,18 @@
     for off in range(1, peers):
         stat_copy(off).start()
     stat_recv[my_head] = stat_send[...]
-    forward.wait_l(half)
+
+    @pl.when(jnp.logical_not(at_start))
+    def _():
+        pl.semaphore_wait(tokens_sem.at[0], 1)
+        pass_up()
+
+    @pl.when(jnp.logical_not(at_end))
+    def _():
+        pl.semaphore_wait(tokens_sem.at[1], 1)
+        pass_down()
+
+    forward.sent()
     backward.start()
     many = stat_recv.at[0 : peers - 1]
     remote(many, many, stat_sem.at[0], stat_sem.at[1], "head", lax.rem(my_head + 1, peers)).wait_recv()
@@ -406,8 +457,8 @@
                 right = jnp.concatenate([right, ts[h, j]], axis=0)
             q[h, span] = mm(left, right, AB).astype(BF16)
 
-    def keep_out(h, state):
-        r_out[h] = state.astype(BF16)
+    def keep_out(h, piece, state):
+        r_out[h, piece] = state.astype(BF16)
 
     def gain_copy(off):
         return remote(
@@ -415,32 +466,30 @@
         )
 
     def normalize_pair(i):
-        normalize(2 * i)
-        normalize(2 * i + 1)
-        backward.copy_l(backward.other(i)).start()
-
-    loop(half, normalize_pair)
+        normalize(2 * i + 2)
+        normalize(2 * i + 3)
+        backward.give(i + 1)
+
+    normalize(backward.other(0))
+    backward.give(0)
+    normalize(backward.led(0))
+    loop(half - 1, normalize_pair)
     for off in range(1, n):
         gain_copy(off).start()
-    back_lag = jnp.maximum(3 * backward.row - 1, 0)
+    back_lag = jnp.minimum(6 * backward.row, heads)
 
     def backward_turn(i):
         at = i - back_lag
 
         @pl.when(jnp.logical_and(at >= 0, at < half))
         def _():
-            backward.step(backward.led(at), keep_out)
-
-        @pl.when(i < half)
+            backward.step(at, keep_out)
+
+        @pl.when(i < heads)
         def _():
-            loop(2, lambda o: gradients(2 * i + o))
-
-    loop(half + back_lag, backward_turn)
-
-    def backward_take(s):
-        backward.take(backward.other(s), keep_out)
-
-    loop(half, backward_take)
+            gradients(i)
+
+    loop(jnp.maximum(heads, half + back_lag), backward_turn)
 
     gain_recv[me] = gain_send[...]
     many_gains = gain_recv.at[0 : n - 1]
@@ -450,10 +499,12 @@
         gain_total = gain_total + gain_recv[i]
     gg_out[...] = gain_total
 
+    def backward_take(s):
+        backward.take(s, keep_out)
+
+    loop(half, backward_take)
     pair_copy().wait_send()
-    forward.wait_xz(half)
-    backward.wait_l(half)
-    backward.wait_xz(half)
+    backward.sent()
     remote(many, many, stat_sem.at[0], stat_sem.at[1], "head", lax.rem(my_head + 1, peers)).wait_send()
     remote(many_gains, many_gains, gain_sem.at[0], gain_sem.at[1], "seq", forward.partner).wait_send()
 
@@ -517,16 +568,18 @@
             pltpu.VMEM((heads, DH, DH), BF16),
             pltpu.VMEM((4, chunks, heads, DH), F32), pltpu.VMEM((heads, DH), F32),
         ),
-        in_specs=[anywhere] * 4 + [vmem] * 2,
+        in_specs=[anywhere] * 6,
         out_specs=(vmem,) * 9,
         scratch_shapes=[
             *[by_head(BF16)] * 4, states, states, pltpu.VMEM((tokens, depth), BF16),
+            pltpu.VMEM((heads, tokens), F32), pltpu.VMEM((heads, DH), F32),
             per_head(DH, DH), flat, flat, flat, flat,
             pltpu.VMEM((heads, DH), F32), pltpu.VMEM((heads, DH), F32),
             pltpu.VMEM((stat_rows, DH), F32), pltpu.VMEM((peers, stat_rows, DH), F32),
             pltpu.VMEM((heads, DH), F32), pltpu.VMEM((n, heads, DH), F32),
-            *[per_head(DH, DH)] * 6,
-            dma((2, heads // 2)), dma, dma((3, heads)), dma((2, 3)), dma((2,)), dma((2,)), dma((2,)),
+            per_head(DH, DH), *[pltpu.VMEM((heads // 2, DH, DH), F32)] * 5,
+            dma((6,)), dma((2, heads // 2, len(PIECES))), dma((heads // 2,)), dma((3,)),
+            dma((2,)), dma((2,)), dma((2,)), pltpu.SemaphoreType.REGULAR((2,)),
         ],
         compiler_params=pltpu.CompilerParams(
             collective_id=0, has_side_effects=True, vmem_limit_bytes=36 * 1024 * 1024

time: 72.5 us -> 69 us (0.952)
  Pallas kernels: 71.7 us -> 68.2 us
    pallas_call x1, Pallas kernels: 66.8 us -> 63.3 us  [on_device(): pl.pallas_call(functools.partial(main_kernel, n, peers), out_shape=(by_he...]
where the time goes in v2:
time: 69 us; the launch traced here: 68.9 us
  Pallas kernels  68.2 us (99%)
    pallas_call x1, Pallas kernels, on_device(): pl.pallas_call(functools.partial(main_kernel, n, peers), out_shape=(by_he...  63.3 us
    pallas_call x1, Pallas kernels, on_device(): pl.pallas_call(last_kernel, out_shape=(rows,) * 4 + (gains,), in_specs=[v...  4.9 us

profile of v2, /device:TPU:0, one launch (start us, length us, event | category | flops | bytes accessed | tf_op | source)
XLA Modules:
  0.0 68.9 jit_solution(7511022890950562454)
XLA Ops:
  0.6 63.3 %forward_chain.1 = (bf16[16,768,128]{2,1,0:T(8,128)(2,1)S(1)}, bf16[16,768,128]{2,1,0:T(8,128)(2,1)S(1)}, bf16[16,768,128]{2,1,0:T(8,128)(2,1)S(1)}, bf16[16,768...) custom-call(bf16[768,2048]{1,0:T(8,128)(2,1)} %q_hbm.1, ...), custom_call_target="tpu_custom_call" | custom-call | tf_op jit(solution)/shard_map/forward_chain/pallas_call | solution.py:564
  64.0 4.9 %last_terms.1 = (bf16[768,2048]{1,0:T(8,128)(2,1)}, bf16[768,2048]{1,0:T(8,128)(2,1)}, bf16[768,2048]{1,0:T(8,128)(2,1)}, bf16[768,2048]{1,0:T(8,128)(2,1)}, f32[16,128]{1,0:T(8,128)}) custom-call(bf16[16,768,128]{2,1,0:T(8,128)(2,1)S(1)} %get-tuple-element.19.gv, bf16[16,768,128]{2,1,0:T(8,128)(2,1)S(1)} %get-tuple-element.20.gq, ...), custom_call_target="tpu_custom_call" | custom-call | tf_op jit(solution)/shard_map/last_terms/pallas_call | solution.py:589

commit v3 on v2

--- a/solution.py
+++ b/solution.py
@@ -193,7 +193,7 @@
     q, k, kd, g, att, obuf, r_out, rows, gg_out,
     v, qd, ga, wt, qs, ts, columns, ld, gain_ref, state_in, sq_acc, in_acc, inv_b, cen_b,
     whole, partner_whole,
-    stat_send, stat_recv, gain_send, gain_recv,
+    stat_send, stat_recv, gain_send, gain_pair_recv, gain_sum, gain_recv,
     lsend, lrecv, zsend, zrecv, xsend, xrecv,
     once_sem, recv_sems, x_sems, send_sems, pair_sem, stat_sem, gain_sem, tokens_sem,
 ):
@@ -460,10 +460,25 @@
     def keep_out(h, piece, state):
         r_out[h, piece] = state.astype(BF16)
 
-    def gain_copy(off):
-        return remote(
-            gain_send, gain_recv.at[me], gain_sem.at[0], gain_sem.at[1], "seq", lax.rem(me + off, n),
-        )
+    def gain_pair():
+        return remote(gain_send, gain_pair_recv, gain_sem.at[0], gain_sem.at[1], "seq", forward.partner)
+
+    def gain_copy(target):
+        return remote(gain_sum, gain_recv.at[me // 2], gain_sem.at[2], gain_sem.at[3], "seq", target)
+
+    def send_gains(sign):
+        for k in range(1, n // 2):
+            target = me + 2 * k * sign
+
+            @pl.when(jnp.logical_and(target >= 0, target < n))
+            def _():
+                gain_copy(lax.rem(target + n, n)).start()
+
+    def sum_pair():
+        gain_pair().wait_recv()
+        gain_sum[...] = gain_send[...] + gain_pair_recv[...]
+        gain_recv[me // 2] = gain_sum[...]
+        send_gains(1)
 
     def normalize_pair(i):
         normalize(2 * i + 2)
@@ -474,8 +489,7 @@
     backward.give(0)
     normalize(backward.led(0))
     loop(half - 1, normalize_pair)
-    for off in range(1, n):
-        gain_copy(off).start()
+    gain_pair().start()
     back_lag = jnp.minimum(6 * backward.row, heads)
 
     def backward_turn(i):
@@ -489,13 +503,17 @@
         def _():
             gradients(i)
 
+        @pl.when(i == heads - 1)
+        def _():
+            sum_pair()
+
     loop(jnp.maximum(heads, half + back_lag), backward_turn)
 
-    gain_recv[me] = gain_send[...]
-    many_gains = gain_recv.at[0 : n - 1]
-    remote(many_gains, many_gains, gain_sem.at[0], gain_sem.at[1], "seq", forward.partner).wait_recv()
+    send_gains(-1)
+    many_gains = gain_recv.at[0 : n // 2 - 1]
+    remote(many_gains, many_gains, gain_sem.at[2], gain_sem.at[3], "seq", forward.partner).wait_recv()
     gain_total = gain_recv[0]
-    for i in range(1, n):
+    for i in range(1, n // 2):
         gain_total = gain_total + gain_recv[i]
     gg_out[...] = gain_total
 
@@ -506,7 +524,8 @@
     pair_copy().wait_send()
     backward.sent()
     remote(many, many, stat_sem.at[0], stat_sem.at[1], "head", lax.rem(my_head + 1, peers)).wait_send()
-    remote(many_gains, many_gains, gain_sem.at[0], gain_sem.at[1], "seq", forward.partner).wait_send()
+    gain_pair().wait_send()
+    remote(many_gains, many_gains, gain_sem.at[2], gain_sem.at[3], "seq", forward.partner).wait_send()
 
 
 def last_kernel(
@@ -576,10 +595,10 @@
             per_head(DH, DH), flat, flat, flat, flat,
             pltpu.VMEM((heads, DH), F32), pltpu.VMEM((heads, DH), F32),
             pltpu.VMEM((stat_rows, DH), F32), pltpu.VMEM((peers, stat_rows, DH), F32),
-            pltpu.VMEM((heads, DH), F32), pltpu.VMEM((n, heads, DH), F32),
+            *[pltpu.VMEM((heads, DH), F32)] * 3, pltpu.VMEM((n // 2, heads, DH), F32),
             per_head(DH, DH), *[pltpu.VMEM((heads // 2, DH, DH), F32)] * 5,
             dma((6,)), dma((2, heads // 2, len(PIECES))), dma((heads // 2,)), dma((3,)),
-            dma((2,)), dma((2,)), dma((2,)), pltpu.SemaphoreType.REGULAR((2,)),
+            dma((2,)), dma((2,)), dma((4,)), pltpu.SemaphoreType.REGULAR((2,)),
         ],
         compiler_params=pltpu.CompilerParams(
             collective_id=0, has_side_effects=True, vmem_limit_bytes=36 * 1024 * 1024

time: 69 us -> 68.1 us (0.987)
  Pallas kernels: 68.2 us -> 67.3 us
    pallas_call x1, Pallas kernels: 63.3 us -> 62.4 us  [on_device(): pl.pallas_call(functools.partial(main_kernel, n, peers), out_shape=(by_he...]
where the time goes in v3:
time: 68.1 us; the launch traced here: 67.9 us
  Pallas kernels  67.3 us (99%)
    pallas_call x1, Pallas kernels, on_device(): pl.pallas_call(functools.partial(main_kernel, n, peers), out_shape=(by_he...  62.4 us
    pallas_call x1, Pallas kernels, on_device(): pl.pallas_call(last_kernel, out_shape=(rows,) * 4 + (gains,), in_specs=[v...  4.9 us

profile of v3, /device:TPU:0, one launch (start us, length us, event | category | flops | bytes accessed | tf_op | source)
XLA Modules:
  0.0 67.9 jit_solution(16003414830237889979)
XLA Ops:
  0.6 62.4 %forward_chain.1 = (bf16[16,768,128]{2,1,0:T(8,128)(2,1)S(1)}, bf16[16,768,128]{2,1,0:T(8,128)(2,1)S(1)}, bf16[16,768,128]{2,1,0:T(8,128)(2,1)S(1)}, bf16[16,768...) custom-call(bf16[768,2048]{1,0:T(8,128)(2,1)} %q_hbm.1, ...), custom_call_target="tpu_custom_call" | custom-call | tf_op jit(solution)/shard_map/forward_chain/pallas_call | solution.py:583
  63.0 4.9 %last_terms.1 = (bf16[768,2048]{1,0:T(8,128)(2,1)}, bf16[768,2048]{1,0:T(8,128)(2,1)}, bf16[768,2048]{1,0:T(8,128)(2,1)}, bf16[768,2048]{1,0:T(8,128)(2,1)}, f32[16,128]{1,0:T(8,128)}) custom-call(bf16[16,768,128]{2,1,0:T(8,128)(2,1)S(1)} %get-tuple-element.19.gv, bf16[16,768,128]{2,1,0:T(8,128)(2,1)S(1)} %get-tuple-element.20.gq, ...), custom_call_target="tpu_custom_call" | custom-call | tf_op jit(solution)/shard_map/last_terms/pallas_call | solution.py:608

commit v4 on v3

--- a/solution.py
+++ b/solution.py
@@ -141,7 +141,7 @@
         for i in range(len(PIECES)):
             self.copy_l(s, i).start()
 
-    def step(self, s, take):
+    def step(self, s, take, send_x=True):
         h = self.led(s)
         own, theirs = self.whole[pl.ds(h, 1), :], self.partner_whole[pl.ds(h, 1), :]
         for i, piece in enumerate(PIECES):
@@ -170,7 +170,8 @@
             def _():
                 self.copy_z(s, i).start()
 
-        self.copy_x(s).start()
+        if send_x:
+            self.copy_x(s).start()
 
     def take(self, s, take):
         self.copy_x(s).wait_recv()
@@ -293,7 +294,19 @@
     pl.when(at_end)(pass_down)
     local_states([forward.led(0)])
 
+    def keep_in(h, piece, state):
+        state_in[h, piece] = state
+
     def local_rest(i):
+        @pl.when(i == half - 2)
+        def _():
+            pair_copy().wait_recv()
+            gain_in.wait()
+
+        @pl.when(jnp.logical_and(i == half - 2, forward.first))
+        def _():
+            forward.step(0, keep_in, send_x=False)
+
         local_states([2 * i + 2, 2 * i + 3])
         forward.give(i + 1)
 
@@ -327,30 +340,27 @@
             sq_acc[span] += value * value
             in_acc[span] += g[h, span].astype(F32) * gain * value
 
-    def keep_in(h, piece, state):
-        state_in[h, piece] = state
 
     sq_acc[...] = jnp.zeros_like(sq_acc)
     in_acc[...] = jnp.zeros_like(in_acc)
-    pair_copy().wait_recv()
-    gain_in.wait()
+    pl.when(forward.first)(lambda: forward.copy_x(0).start())
     landed(q, heads, once_sem.at[3])
     landed(g, heads, once_sem.at[0])
-    lag = jnp.minimum(4 * forward.row, half)
+    lag = jnp.minimum(3 * forward.row, half)
 
     def forward_turn(i):
         at = i - lag
-        ready = jnp.logical_and(at >= 0, at < half)
-
-        @pl.when(ready)
-        def _():
-            forward.step(at, keep_in)
+        turn = at + jnp.where(forward.first, 1, 0)
+
+        @pl.when(jnp.logical_and(turn >= 0, turn < half))
+        def _():
+            forward.step(turn, keep_in)
 
         @pl.when(i < half)
         def _():
             intra_pair(i)
 
-        @pl.when(ready)
+        @pl.when(jnp.logical_and(at >= 0, at < half))
         def _():
             arrive(forward.led(at))
 

time: 68.1 us -> 67.5 us (level)
  no operation moved by 1% of the time
where the time goes in v4:
time: 67.5 us; the launch traced here: 67.4 us
  Pallas kernels  66.8 us (99%)
    pallas_call x1, Pallas kernels, on_device(): pl.pallas_call(functools.partial(main_kernel, n, peers), out_shape=(by_he...  61.9 us
    pallas_call x1, Pallas kernels, on_device(): pl.pallas_call(last_kernel, out_shape=(rows,) * 4 + (gains,), in_specs=[v...  4.9 us

profile of v4, /device:TPU:0, one launch (start us, length us, event | category | flops | bytes accessed | tf_op | source)
XLA Modules:
  0.0 67.4 jit_solution(7449041435292976657)
XLA Ops:
  0.6 61.9 %forward_chain.1 = (bf16[16,768,128]{2,1,0:T(8,128)(2,1)S(1)}, bf16[16,768,128]{2,1,0:T(8,128)(2,1)S(1)}, bf16[16,768,128]{2,1,0:T(8,128)(2,1)S(1)}, bf16[16,768...) custom-call(bf16[768,2048]{1,0:T(8,128)(2,1)} %q_hbm.1, ...), custom_call_target="tpu_custom_call" | custom-call | tf_op jit(solution)/shard_map/forward_chain/pallas_call | solution.py:593
  62.5 4.9 %last_terms.1 = (bf16[768,2048]{1,0:T(8,128)(2,1)}, bf16[768,2048]{1,0:T(8,128)(2,1)}, bf16[768,2048]{1,0:T(8,128)(2,1)}, bf16[768,2048]{1,0:T(8,128)(2,1)}, f32[16,128]{1,0:T(8,128)}) custom-call(bf16[16,768,128]{2,1,0:T(8,128)(2,1)S(1)} %get-tuple-element.19.gv, bf16[16,768,128]{2,1,0:T(8,128)(2,1)S(1)} %get-tuple-element.20.gq, ...), custom_call_target="tpu_custom_call" | custom-call | tf_op jit(solution)/shard_map/last_terms/pallas_call | solution.py:618
